TPU v7x, 32 devices: a whole 2x2x4 slice. The times are simulated.
32 devices in a mesh: img: 8 (over z, y), sp: 4 (over x, core).
Axes of the slice: x: 2, y: 2, z: 4, core: 2. Of those that a mesh axis runs over, the one named last changes fastest.
Arguments:
- patches: bfloat16 [4096, 1280], P(('img', 'sp')), parts along dimension 0, may hold values from -6 to 6
- pos_ids: int32 [2, 4096], P(None, 'img'), parts along dimension 1, may hold values from 0 to 31, as said below
- norm_gain: float32 [1280], replicated, may hold values from 0.5 to 1.5
- norm_bias: float32 [1280], replicated, may hold values from -3 to 3
- qkv_weight: bfloat16 [1280, 3, 1280], P(None, None, 'sp')
- qkv_bias: float32 [3, 1280], replicated, may hold values from -3 to 3
- proj_weight: bfloat16 [1280, 1280], P('sp'), may hold values from -0.15625 to 0.15625
- proj_bias: float32 [1280], replicated, may hold values from -3 to 3
- merge_gain: float32 [1280], replicated, may hold values from 0.5 to 1.5
- merge_bias: float32 [1280], replicated, may hold values from -3 to 3
- fc1_weight: bfloat16 [5120, 5120], P(None, 'sp'), may hold values from -0.078125 to 0.078125
- fc1_bias: float32 [5120], P('sp'), may hold values from -3 to 3
Outputs:
- vit_out: bfloat16 [4096, 1280], P(('img', 'sp')), parts along dimension 0
- merged_hidden: bfloat16 [1024, 5120], P('img', 'sp'), parts along dimension 0
There are 8 independent parts, one for each index of `img`. A program takes and returns all parts, laid end to end along the dimension named above; an argument that names none is the same for every part. Nothing has to cross between parts.
Inputs may be any that keep to these rules, and one draw needn't show every extreme that they name: pos_ids[0] and pos_ids[1] are the row and column of each patch on a grid of 2 R by 2 C patches, where the grid of 2x2 blocks has R rows and C columns, R C = 128, and one of R and C equals min(8, 128); each aligned run of 4 patches is one 2x2 block in row-major order inside it; every block of the grid appears once, in the order that the argument gives.
All inputs are finite; a program needn't handle non-finite values.
Results may differ from a plain program's by a relative error of at most 0.006.
Values may be sent and summed in bfloat16 or wider, within the bound.
A program may use at most 64 MiB of HBM per device.

v0:
```python
import jax
import jax.numpy as jnp
from jax import lax
from jax.sharding import PartitionSpec as P

HEADS = 16


def layer_norm(values, gain, bias):
    mean = jnp.mean(values, axis=-1, keepdims=True)
    centered = values - mean
    var = jnp.mean(centered * centered, axis=-1, keepdims=True)
    return centered * lax.rsqrt(var + 1e-06) * gain + bias


def rotate(values, positions, nheads):
    count = values.shape[0]
    hdim = values.shape[1] // nheads
    quarter = hdim // 4
    inv = 1.0 / 10000.0 ** (jnp.arange(quarter, dtype=jnp.float32) * 2.0 / (hdim // 2))
    rows = positions[0].astype(jnp.float32)[:, None] * inv
    cols = positions[1].astype(jnp.float32)[:, None] * inv
    angle = jnp.concatenate([rows, cols, rows, cols], axis=1)
    cosine = jnp.cos(angle)[:, None, :]
    sine = jnp.sin(angle)[:, None, :]
    shaped = values.reshape(count, nheads, hdim)
    half = hdim // 2
    turned = jnp.concatenate([-shaped[..., half:], shaped[..., :half]], axis=-1)
    return (shaped * cosine + turned * sine).reshape(count, nheads * hdim)


def attend(query, keys, value, nheads, hdim):
    count = query.shape[0]
    block = min(512, count)
    qblocks = query.reshape(count // block, block, nheads, hdim)
    kshaped = keys.reshape(count, nheads, hdim)
    vshaped = value.reshape(count, nheads, hdim)
    scale = 1.0 / jnp.sqrt(jnp.float32(hdim))

    def one_block(qpart):
        scores = (
            jnp.einsum("bhd,khd->hbk", qpart, kshaped, preferred_element_type=jnp.float32) * scale
        )
        top = jnp.max(scores, axis=-1, keepdims=True)
        expo = jnp.exp(scores - top)
        weights = (expo / jnp.sum(expo, axis=-1, keepdims=True)).astype(jnp.bfloat16)
        result = jnp.einsum("hbk,khd->bhd", weights, vshaped, preferred_element_type=jnp.float32)
        return result.astype(jnp.bfloat16).reshape(block, nheads * hdim)

    return lax.map(one_block, qblocks).reshape(count, nheads * hdim)


def per_device(
    patches,
    pos_ids,
    norm_gain,
    norm_bias,
    qkv_weight,
    qkv_bias,
    proj_weight,
    proj_bias,
    merge_gain,
    merge_bias,
    fc1_weight,
    fc1_bias,
):
    groups = lax.axis_size("sp")
    where = lax.axis_index("sp")
    prow = patches.shape[0]
    width = patches.shape[1]
    heads_local = HEADS // groups
    hdim = width // HEADS
    local_width = width // groups
    xfloat = patches.astype(jnp.float32)
    normed = layer_norm(xfloat, norm_gain, norm_bias).astype(jnp.bfloat16)
    bias_local = lax.dynamic_slice_in_dim(qkv_bias, where * local_width, local_width, 1)
    qkv = (
        jnp.einsum(
            "pd,dcn->pcn",
            lax.all_gather(normed, "sp", axis=0, tiled=True),
            qkv_weight,
            preferred_element_type=jnp.float32,
        )
        + bias_local[None]
    )
    query = rotate(qkv[:, 0], pos_ids, heads_local).astype(jnp.bfloat16)
    keys = rotate(qkv[:, 1], pos_ids, heads_local).astype(jnp.bfloat16)
    value = qkv[:, 2].astype(jnp.bfloat16)
    spread = jnp.stack([query, keys, value])
    attended = attend(spread[0], spread[1], spread[2], heads_local, hdim)
    returned = lax.all_to_all(attended, "sp", split_axis=0, concat_axis=1, tiled=True)
    projected = jnp.dot(
        returned,
        lax.all_gather(proj_weight, "sp", axis=0, tiled=True),
        preferred_element_type=jnp.float32,
    )
    vit_out = (xfloat + projected + proj_bias).astype(jnp.bfloat16)
    zn = layer_norm(vit_out.astype(jnp.float32), merge_gain, merge_bias).astype(jnp.bfloat16)
    blocks = zn.reshape(prow // 4, 4 * width)
    hidden = (
        jnp.dot(
            lax.all_gather(blocks, "sp", axis=0, tiled=True),
            fc1_weight,
            preferred_element_type=jnp.float32,
        )
        + fc1_bias
    )
    merged_hidden = jax.nn.gelu(hidden, approximate=False).astype(jnp.bfloat16)
    return (vit_out, merged_hidden)


def solution(mesh):
    return jax.shard_map(
        per_device,
        mesh=mesh,
        in_specs=(
            P(("img", "sp"), None),
            P(None, "img"),
            P(),
            P(),
            P(None, None, "sp"),
            P(),
            P("sp", None),
            P(),
            P(),
            P(),
            P(None, "sp"),
            P("sp"),
        ),
        out_specs=(P(("img", "sp"), None), P("img", "sp")),
        check_vma=False,
    )
```

profile of v0, /device:TPU:0, one launch (start us, length us, event | category | flops | bytes accessed | tf_op | source)
XLA Modules:
  0.0 105.2 jit_solution(13298240738997939612)
XLA Ops:
  7.2 0.0 copy-start
  7.2 0.0 all-gather.4.cloned.1.call-start
  7.2 1.2 %convert_reduce_fusion = f32[128]{0:T(128)S(1)} fusion(bf16[128,1280]{1,0:T(8,128)(2,1)} %param.12), kind=kLoop, calls=%fused_computation.17 | loop fusion | flops 327552 | bytes 328192 | tf_op jit(solution)/shard_map/reduce_sum | solution.py:10
  8.5 1.2 %fusion.15 = f32[128]{0:T(128)S(1)} fusion(bf16[128,1280]{1,0:T(8,128)(2,1)} %param.12, f32[128]{0:T(128)S(1)} %broadcast_multiply_fusion.3), kind=kLoop, calls=%fused_computation.24 | loop fusion | flops 655232 | bytes 328704 | tf_op jit(solution)/shard_map/reduce_sum | solution.py:12
  9.7 2.0 %fusion.18 = bf16[128,1280]{1,0:T(8,128)(2,1)} fusion(bf16[128,1280]{1,0:T(8,128)(2,1)} %param.12, f32[1280]{0:T(1024)} %param.15, f32[1280]{0:T(1024)} %param.14, f32[128]{0:T(128)S(1)} %add_rsqrt_fusion.1, f32[128]{0:T(128)S(1)} %broadcast_multiply_fusion.3), kind=kLoop, calls=%fused_computation.27 | loop fusion | flops 983040 | bytes 666624 | tf_op jit(solution)/shard_map/convert_element_type | solution.py:75
  11.7 0.0 all-gather.4.cloned.1.call-update
  11.7 0.0 all-gather.6.cloned.1.call-start
  11.8 0.7 all-gather.6.cloned.1.call-update
  12.5 0.0 all-gather.8.cloned.1.call-start
  12.5 0.8 constant_dynamic-slice_fusion
  13.3 0.8 slice_convert_fusion.2
  14.1 0.1 broadcast_multiply_fusion.1
  14.2 0.6 fusion.40
  14.7 18.0 %all-gather.4.cloned.1.call-done = bf16[512,1280]{1,0:T(8,128)(2,1)} async-done(((bf16[128,1280]{1,0:T(8,128)(2,1)}), bf16[512,1280]{1,0:T(8,128)(2,1)}) %all-gather.4.cloned.1.call-update) | async-done | bytes 1310736 | tf_op jit(solution)/shard_map/all_gather | solution.py:80
  32.8 2.8 %convolution_add_fusion.2 = f32[512,3,320]{0,2,1:T(8,128)S(1)} fusion(bf16[1280,3,320]{0,2,1:T(8,128)(2,1)S(1)} %copy-done, bf16[512,1280]{1,0:T(8,128)(2,1)} %all-gather.4.cloned.1.call-done, f32[3,320]{1,0:T(4,128)S(1)} %constant_dynamic-slice_fusion), kind=kOutput, calls=%fused_computation.11 | convolution fusion | flops 1258782720 | bytes 5738240 | tf_op jit(solution)/shard_map/pd,dcn->pcn/dot_general | solution.py:78
  35.5 0.8 slice.51
  36.3 0.1 fusion.42
  36.4 0.1 slice_negate_fusion
  36.6 0.4 fusion.29
  37.0 3.4 %fusion.43 = (f32[4,512]{1,0:T(4,128)S(1)}, f32[4,512,512]{1,2,0:T(8,128)}) fusion(bf16[512,4,80]{0,2,1:T(8,128)(2,1)S(1)} %get-tuple-element.24, bf16[512,4,80]{0,2,1:T(8,128)(2,1)S(1)} %get-tuple-element.23), kind=kOutput, calls=%fused_computation.75 | convolution fusion | flops 170918400 | bytes 4857856 | tf_op jit(solution)/shard_map/while/body/eval_jaxpr/sub | solution.py:45
  40.4 3.1 %fusion.10 = bf16[512,4,80]{0,2,1:T(8,128)(2,1)S(1)} fusion(bf16[512,4,80]{0,2,1:T(8,128)(2,1)S(1)} %bitcast.30, f32[4,512,512]{1,2,0:T(8,128)} %get-tuple-element.32, f32[4,512]{1,0:T(4,128)S(1)} %get-tuple-element.31), kind=kOutput, calls=%fused_computation.14 | convolution fusion | flops 170033152 | bytes 4857856 | tf_op jit(solution)/shard_map/while/body/eval_jaxpr/hbk,khd->bhd/dot_general | solution.py:47
  43.5 0.1 all_to_all.14
  43.6 13.0 %all_to_all.19 = bf16[4,128,320]{1,2,0:T(8,128)(2,1)S(1)} all-to-all(bf16[4,128,320]{1,2,0:T(8,128)(2,1)S(1)} %copy.16), channel_id=1, replica_groups=mesh['img'=8,'sp'=4] {'sp'}, dimensions={0} | all-to-all | bytes 655360 | tf_op jit(solution)/shard_map/all_to_all | solution.py:91
  56.6 10.5 %all-gather.6.cloned.1.call-done = bf16[1280,1280]{1,0:T(8,128)(2,1)} async-done(((bf16[320,1280]{1,0:T(8,128)(2,1)}), bf16[1280,1280]{1,0:T(8,128)(2,1)}) %all-gather.6.cloned.1.call-update) | async-done | bytes 3276816 | tf_op jit(solution)/shard_map/all_gather | solution.py:94
  67.1 2.7 %convert_reduce_fusion.1 = (f32[128]{0:T(128)S(1)}, bf16[128,1280]{1,0:T(8,128)(2,1)S(1)}) fusion(f32[1280]{0:T(1024)S(1)} %copy-done.4, bf16[128,1280]{0,1:T(8,128)(2,1)S(1)} %bitcast.29, bf16[1280,1280]{1,0:T(8,128)(2,1)} %all-gather.6.cloned.1.call-done, bf16[128,1280]{1,0:T(8,128)(2,1)S(1)} %copy-done.1), kind=kOutput, calls=%fused_computation.19 | convolution fusion | flops 420413312 | bytes 4265472 | tf_op jit(solution)/shard_map/dot_general | solution.py:92
  69.8 0.0 copy-start.2
  69.8 0.2 fusion.19
  70.1 0.3 fusion.22
  70.4 0.9 reshape.180
  71.3 0.0 all-gather.8.cloned.1.call-update
  71.3 18.3 %all-gather.8.cloned.1.call-done = bf16[128,5120]{1,0:T(8,128)(2,1)} async-done(((bf16[32,5120]{1,0:T(8,128)(2,1)}), bf16[128,5120]{1,0:T(8,128)(2,1)}) %all-gather.8.cloned.1.call-update) | async-done | bytes 1310736 | tf_op jit(solution)/shard_map/all_gather | solution.py:102
  89.6 9.1 %fusion.25 = bf16[128,1280]{1,0:T(8,128)(2,1)} fusion(bf16[128,5120]{1,0:T(8,128)(2,1)} %all-gather.8.cloned.1.call-done, bf16[5120,1280]{1,0:T(8,128)(2,1)} %param.22, f32[1280]{0:T(1024)S(1)} %copy-done.7), kind=kOutput, calls=%fused_computation.34 | convolution fusion | flops 1688535040 | bytes 14750720 | tf_op jit(solution)/shard_map/dot_general | solution.py:101
  (20 shorter events, 0.1 us)
Async XLA Ops:
  7.2 25.6 %copy-start = (bf16[1280,3,320]{0,2,1:T(8,128)(2,1)S(1)}, bf16[1280,3,320]{0,2,1:T(8,128)(2,1)}, u32[]{:S(2)}) copy-start(bf16[1280,3,320]{0,2,1:T(8,128)(2,1)} %param.16) | copy-start | bytes 7372804
  7.2 25.6 %all-gather.4.cloned.1.call-start = ((), (), s32[]{:S(2)}) async-start(), calls=%async_computation.1 | async-start | bytes 1638400 | tf_op jit(solution)/shard_map/all_gather | solution.py:80
  11.7 55.4 %all-gather.6.cloned.1.call-start = ((), (), s32[]{:S(2)}) async-start(), calls=%async_computation.2 | async-start | bytes 4096000 | tf_op jit(solution)/shard_map/all_gather | solution.py:94
  12.5 77.2 %all-gather.8.cloned.1.call-start = ((), (), s32[]{:S(2)}) async-start(), calls=%async_computation.3 | async-start | bytes 1638400 | tf_op jit(solution)/shard_map/all_gather | solution.py:102
  36.9 3.5 %copy-start.3 = (bf16[512,1,320]{0,2,1:T(8,128)(2,1)S(1)}, bf16[512,1,320]{0,2,1:T(8,128)(2,1)}, u32[]{:S(2)}) copy-start(bf16[512,1,320]{0,2,1:T(8,128)(2,1)} %slice.51) | copy-start | bytes 983044
  40.4 26.7 %copy-start.1 = (bf16[128,1280]{1,0:T(8,128)(2,1)S(1)}, bf16[128,1280]{1,0:T(8,128)(2,1)}, u32[]{:S(2)}) copy-start(bf16[128,1280]{1,0:T(8,128)(2,1)} %param.12) | copy-start | bytes 983044
  40.4 26.7 %copy-start.4 = (f32[1280]{0:T(1024)S(1)}, f32[1280]{0:T(1024)}, u32[]{:S(2)}) copy-start(f32[1280]{0:T(1024)} %param.19) | copy-start | bytes 15364
  43.5 26.6 %copy-start.5 = (f32[1280]{0:T(1024)S(1)}, f32[1280]{0:T(1024)}, u32[]{:S(2)}) copy-start(f32[1280]{0:T(1024)} %param.21) | copy-start | bytes 15364
  43.5 26.6 %copy-start.6 = (f32[1280]{0:T(1024)S(1)}, f32[1280]{0:T(1024)}, u32[]{:S(2)}) copy-start(f32[1280]{0:T(1024)} %param.20) | copy-start | bytes 15364
  56.6 33.0 %copy-start.7 = (f32[1280]{0:T(1024)S(1)}, f32[1280]{0:T(1024)}, u32[]{:S(2)}) copy-start(f32[1280]{0:T(1024)} %param.23) | copy-start | bytes 15364
  69.8 28.9 %copy-start.2 = (bf16[128,1280]{1,0:T(8,128)(2,1)}, bf16[128,1280]{1,0:T(8,128)(2,1)S(1)}, u32[]{:S(2)}) copy-start(bf16[128,1280]{1,0:T(8,128)(2,1)S(1)} %get-tuple-element.34) | copy-start | bytes 983044
Sparse Core Ops, SparseCore 0:
  11.8 20.8 all-gather.3
  34.3 32.7 all-gather.5
  71.4 18.1 all-gather.7
where the time goes:
time: 106 us; the launch traced here: 105 us
  waiting for transfers between devices  47.5 us (45%)
  matrix products  21 us (20%)
  between operations  13.9 us (13%)
  blocking collectives  13 us (12%)
  other arithmetic  6.95 us (7%)
  local copies, waits for them, and re-layouts  2.74 us (3%)
    all_gather x1, waiting for transfers between devices, per_device(): lax.all_gather(blocks, 'sp', axis=0, tiled=True)  18.3 us
    all_gather x1, waiting for transfers between devices, per_device(): lax.all_gather(normed, 'sp', axis=0, tiled=True)  18 us
    all_to_all x1, blocking collectives, per_device(): lax.all_to_all(attended, 'sp', split_axis=0, concat_axis=1, tiled=True)  13 us
    all_gather x1, waiting for transfers between devices, per_device(): lax.all_gather(proj_weight, 'sp', axis=0, tiled=True)  10.5 us
    dot_general x1, matrix products, per_device(): jnp.dot(lax.all_gather(blocks, 'sp', axis=0, tiled=True), fc1_weight, pre...  9.06 us
    sub x1, matrix products, one_block(): expo = jnp.exp(scores - top)  3.44 us
    dot_general x1, matrix products, one_block(): jnp.einsum('hbk,khd->bhd', weights, vshaped, preferred_element_type=jnp.f...  3.07 us
    dot_general x1, matrix products, per_device(): jnp.einsum('pd,dcn->pcn', lax.all_gather(normed, 'sp', axis=0, tiled=True...  2.77 us
  transfers between devices with their start and end apart: 3, of which 3 were waited for; matrix products, arithmetic and copies ran while one was open for 12% of the time, Pallas kernels for 0%

commit v1 on v0

--- a/solution.py
+++ b/solution.py
@@ -1,9 +1,321 @@
+import functools
+
 import jax
 import jax.numpy as jnp
+import numpy as np
 from jax import lax
+from jax.experimental import pallas as pl
+from jax.experimental.pallas import tpu as pltpu
 from jax.sharding import PartitionSpec as P
 
 HEADS = 16
+MESH = pl.DeviceIdType.MESH
+F32 = jnp.float32
+BF16 = jnp.bfloat16
+
+
+def norm_rows(v, gain, bias):
+    mean = jnp.mean(v, axis=-1, keepdims=True)
+    cen = v - mean
+    var = jnp.mean(cen * cen, axis=-1, keepdims=True)
+    return cen * lax.rsqrt(var + 1e-06) * gain + bias
+
+
+def put(ref, row, v):
+    for t in range(ref.shape[-3]):
+        ref[t, row:row + v.shape[0]] = v[:, t * 128:(t + 1) * 128]
+
+
+def every_fourth(ref, k, n):
+    return jnp.concatenate([ref[t, pl.ds(k, n, stride=4), :] for t in range(ref.shape[-3])], axis=1)
+
+
+def fused_kernel(
+    hdim, x_hbm, pos_ref, inv_ref, g1_ref, b1_ref, wq_hbm, bq_ref, pw_hbm, pb_ref, g2_ref, b2_ref, fw_hbm, fb_ref,
+    vit_ref, out_ref,
+    xb, xf, nf, nall, wq, pw, fw, tab, bqt, qs, ks, vs, att_t, att, att_in, pf, ps, pr, zb, hid, vf,
+    loc, snd, rcv,
+):
+    me = lax.axis_index("sp")
+    chip = me // 2
+    core = me % 2
+    partner = {"sp": me + 1 - 2 * core}
+    peer = {"sp": lax.rem(me + 2, 4)}
+    rows, width = x_hbm.shape
+    half = rows // 2
+    quad = rows // 4
+    lw = pw_hbm.shape[0]
+    nh = lw // hdim
+    hp = qs.shape[2]
+    count = 4 * rows
+    cols = 2 * rows
+    kdim = fw_hbm.shape[0] // 4
+
+    def local(src, dst, i):
+        return pltpu.make_async_copy(src, dst, loc.at[i])
+
+    def remote(src, dst, i, dev):
+        return pltpu.make_async_remote_copy(
+            src_ref=src, dst_ref=dst, send_sem=snd.at[i], recv_sem=rcv.at[i], device_id=dev, device_id_type=MESH
+        )
+
+    lx = local(x_hbm, xb.at[0], 0)
+    lx.start()
+    lq = local(wq_hbm, wq, 1)
+    lq.start()
+    lp = local(pw_hbm, pw.at[0, pl.ds(0, lw)], 2)
+    lp.start()
+    lf = [local(fw_hbm.at[pl.ds(k * kdim, kdim)], fw.at[k], 3 + k) for k in range(4)]
+    for c in lf:
+        c.start()
+
+    barrier = pltpu.get_barrier_semaphore()
+    for dev in (partner, peer):
+        pl.semaphore_signal(barrier, inc=1, device_id=dev, device_id_type=MESH)
+    lx.wait()
+    pl.semaphore_wait(barrier, 2)
+
+    x_half = [
+        remote(xb.at[0, pl.ds(h * half, half)], xb.at[2, pl.ds(h * half, half)], 1 + h, peer) for h in range(2)
+    ]
+    for c in x_half:
+        c.start()
+    x_part = remote(xb.at[0], xb.at[1], 0, partner)
+    x_part.start()
+    fwd = [
+        remote(xb.at[2, pl.ds(h * half, half)], xb.at[3, pl.ds(h * half, half)], 3 + h, partner) for h in range(2)
+    ]
+
+    slot_c = lax.broadcasted_iota(jnp.int32, (count, count), 1)
+    side = slot_c // cols
+    rest = slot_c % cols
+    kk = rest // half
+    cc = (rest % half) // quad
+    bb = rest % quad
+    ch = jnp.where(side == 0, chip, 1 - chip)
+    want = ((2 * ch + cc) * quad + bb) * 4 + kk
+    hot = (want == lax.broadcasted_iota(jnp.int32, (count, count), 0)).astype(F32).astype(BF16)
+    tab[0, 0:8] = jnp.zeros((8, count), F32)
+    tab[0, 0:2] = pos_ref[...].astype(F32)
+    pos = jnp.dot(tab[0, 0:8].astype(BF16), hot, preferred_element_type=F32)
+    th = hdim // 2
+    invc = jnp.transpose(inv_ref[...])
+    angle = invc[0:th, 0:1] * pos[0:1, :] + invc[0:th, 1:2] * pos[1:2, :]
+    tab[0] = jnp.cos(angle)
+    tab[1] = jnp.sin(angle)
+    bqt[...] = jnp.zeros(bqt.shape, F32)
+    bqt[0:3] = bq_ref[...]
+    turned = pltpu.roll(bqt[0:8], lax.rem(width - me * lw, width), 1)
+    bqt[0:8] = turned
+    lwp = att_t.shape[0]
+    bias_t = jnp.transpose(bqt[:, 0:lwp])
+    att_t[...] = jnp.zeros(att_t.shape, F32)
+    pw[0, lw:lwp] = jnp.zeros((lwp - lw, width), BF16)
+    pw[1, lw:lwp] = jnp.zeros((lwp - lw, width), BF16)
+    hid[...] = jnp.zeros(hid.shape, F32)
+    g1 = g1_ref[...].reshape(1, width)
+    b1 = b1_ref[...].reshape(1, width)
+
+    def norm_half(slot, h):
+        v = xb[slot, h * half:(h + 1) * half].astype(F32)
+        if slot % 2 == 0:
+            put(xf.at[slot // 2], h * half, v)
+        put(nf, 0, norm_rows(v, g1, b1))
+        at = core if slot % 2 == 0 else 1 - core
+        for k in range(4):
+            piece = every_fourth(nf, k, half // 4).astype(BF16)
+            start = pl.multiple_of((slot // 2) * cols + k * half + at * quad + h * (quad // 2), quad // 2)
+            nall[pl.ds(start, quad // 2), :] = piece
+
+    def qkv_side(s):
+        n = nall[s * cols:(s + 1) * cols]
+        cos = tab[0, :, s * cols:(s + 1) * cols]
+        sin = tab[1, :, s * cols:(s + 1) * cols]
+        for c in range(3):
+            res = lax.dot_general(
+                wq[c * lw:(c + 1) * lw], n, (((1,), (1,)), ((), ())), preferred_element_type=F32
+            ) + bias_t[0:lw, c:c + 1]
+            for h in range(nh):
+                a = res[h * hdim:h * hdim + th]
+                b = res[h * hdim + th:(h + 1) * hdim]
+                if c == 2:
+                    vs[h, :, s * cols:(s + 1) * cols] = res[h * hdim:(h + 1) * hdim].astype(BF16)
+                    continue
+                full = jnp.concatenate(
+                    [a * cos - b * sin, b * cos + a * sin, jnp.zeros((hp - hdim, cols), F32)], axis=0
+                )
+                if c == 0:
+                    for m in range(2):
+                        qs[m, h, :, s * rows:(s + 1) * rows] = full[:, m * rows:(m + 1) * rows].astype(BF16)
+                else:
+                    ks[h, s * cols:(s + 1) * cols] = jnp.transpose(full).astype(BF16)
+
+    norm_half(0, 0)
+    norm_half(0, 1)
+    lp.wait()
+    p_send = remote(pw.at[0, pl.ds(0, lw)], pw.at[1, pl.ds(0, lw)], 7, partner)
+    p_send.start()
+    x_part.wait_recv()
+    norm_half(1, 0)
+    norm_half(1, 1)
+    lq.wait()
+    qkv_side(0)
+    for h in range(2):
+        x_half[h].wait_recv()
+        fwd[h].start()
+        norm_half(2, h)
+    for h in range(2):
+        fwd[h].wait_recv()
+        norm_half(3, h)
+    qkv_side(1)
+
+    scale = 1.0 / np.sqrt(np.float32(hdim))
+
+    def att_copy(m):
+        return remote(att.at[m], att_in.at[m], 5 + m, partner)
+
+    def attend(m, _):
+        for h in range(nh):
+            s = jnp.dot(ks[h], qs[m, h], preferred_element_type=F32) * scale
+            e = jnp.exp(s - jnp.max(s, axis=0, keepdims=True))
+            w = (e / jnp.sum(e, axis=0, keepdims=True)).astype(BF16)
+            att_t[h * hdim:(h + 1) * hdim] = jnp.dot(vs[h], w, preferred_element_type=F32)
+        att[m] = jnp.transpose(att_t[...]).astype(BF16)
+        att_copy(m).start()
+        return 0
+
+    lax.fori_loop(0, 2, attend, 0)
+    p_send.wait_recv()
+
+    def part_copy(k):
+        return remote(ps.at[k], pr.at[k], 8 + k, peer)
+
+    def project(k, _):
+        m = k // 2
+
+        @pl.when(k % 2 == 0)
+        def _():
+            att_copy(m).wait_recv()
+
+        base = (k % 2) * half + core * quad
+        near = pl.ds(pl.multiple_of(base, quad), quad)
+        far = pl.ds(pl.multiple_of(rows + base, quad), quad)
+        mine = jnp.concatenate([att[m, near], att[m, far]], axis=0)
+        theirs = jnp.concatenate([att_in[m, near], att_in[m, far]], axis=0)
+        res = jnp.dot(mine, pw[0], preferred_element_type=F32) + jnp.dot(theirs, pw[1], preferred_element_type=F32)
+        pf[k] = res
+        ps[k, pl.ds(pl.multiple_of(chip * quad, quad), quad)] = res[0:quad].astype(BF16)
+        ps[k, pl.ds(pl.multiple_of((1 - chip) * quad, quad), quad)] = res[quad:].astype(BF16)
+        part_copy(k).start()
+        return 0
+
+    lax.fori_loop(0, 4, project, 0)
+    pb = pb_ref[...].reshape(1, width)
+    g2 = g2_ref[...].reshape(1, width)
+    b2 = b2_ref[...].reshape(1, width)
+
+    def z_copy(k):
+        mine = pl.ds(pl.multiple_of(core * half, half), half)
+        return remote(zb.at[k, mine], zb.at[k, mine], 12 + k, partner)
+
+    def finish(k, _):
+        @pl.when(k < 4)
+        def _():
+            part_copy(k).wait_recv()
+            for s in range(2):
+                at = chip if s == 0 else 1 - chip
+                got = pr[k, pl.ds(pl.multiple_of(at * quad, quad), quad)].astype(F32)
+                v = every_fourth(xf.at[s], k, quad) + (pf[k, s * quad:(s + 1) * quad] + got) + pb
+                v = v.astype(BF16).astype(F32)
+                if s == 0:
+                    for t in range(vf.shape[0]):
+                        vf[t, pl.ds(k, quad, stride=4), :] = v[:, t * 128:(t + 1) * 128]
+                z = norm_rows(v, g2, b2).astype(BF16)
+                zb[k, pl.ds(pl.multiple_of(core * half + at * quad, quad), quad)] = z
+            z_copy(k).start()
+
+        @pl.when(k > 0)
+        def _():
+            z_copy(k - 1).wait_recv()
+            pltpu.make_async_copy(fw_hbm.at[pl.ds(0, kdim)], fw.at[k - 1], loc.at[3 + k - 1]).wait()
+            hid[...] += jnp.dot(zb[k - 1], fw[k - 1], preferred_element_type=F32)
+
+        return 0
+
+    lax.fori_loop(0, 5, finish, 0)
+    for t in range(vf.shape[0]):
+        vit_ref[:, t * 128:(t + 1) * 128] = vf[t].astype(BF16)
+    h = hid[...] + fb_ref[...].reshape(1, width)
+    res = (0.5 * h * (1.0 + lax.erf(h * np.float32(np.sqrt(0.5))))).astype(BF16)
+    for c in range(2):
+        for p in range(2):
+            out_ref[(2 * p + c) * quad:(2 * p + c + 1) * quad] = res[(2 * c + p) * quad:(2 * c + p + 1) * quad]
+    x_part.wait_send()
+    p_send.wait_send()
+    for c in x_half + fwd:
+        c.wait_send()
+    for m in range(2):
+        att_copy(m).wait_send()
+    for k in range(4):
+        part_copy(k).wait_send()
+        z_copy(k).wait_send()
+
+
+def fused(patches, pos_ids, norm_gain, norm_bias, qkv_weight, qkv_bias, proj_weight, proj_bias,
+          merge_gain, merge_bias, fc1_weight, fc1_bias):
+    rows, width = patches.shape
+    hdim = width // HEADS
+    lw = proj_weight.shape[0]
+    nh = lw // hdim
+    hp = -(-hdim // 128) * 128
+    lwp = -(-lw // 128) * 128
+    half, quad, count = rows // 2, rows // 4, 4 * rows
+    hidden = fc1_weight.shape[1]
+    quarter = hdim // 4
+    steps = 1.0 / np.float32(10000.0) ** (np.arange(quarter, dtype=np.float32) * np.float32(2.0) / (hdim // 2))
+    inv = np.zeros((128, 128), np.float32)
+    inv[0, :quarter] = steps
+    inv[1, quarter:2 * quarter] = steps
+    wq = jnp.transpose(qkv_weight, (1, 2, 0)).reshape(3 * lw, width)
+    vm = pl.BlockSpec(memory_space=pltpu.VMEM)
+    hbm = pl.BlockSpec(memory_space=pl.ANY)
+    V = pltpu.VMEM
+    return pl.pallas_call(
+        functools.partial(fused_kernel, hdim),
+        out_shape=(jax.ShapeDtypeStruct((rows, width), BF16), jax.ShapeDtypeStruct((rows, hidden), BF16)),
+        in_specs=[hbm, vm, vm, vm, vm, hbm, vm, hbm, vm, vm, vm, hbm, vm],
+        out_specs=(vm, vm),
+        scratch_shapes=[
+            V((4, rows, width), BF16),
+            V((2, width // 128, rows, 128), F32),
+            V((width // 128, half, 128), F32),
+            V((count, width), BF16),
+            V((3 * lw, width), BF16),
+            V((2, lwp, width), BF16),
+            V((4, fc1_weight.shape[0] // 4, hidden), BF16),
+            V((2, hdim // 2, count), F32),
+            V((128, width), F32),
+            V((2, nh, hp, 2 * rows), BF16),
+            V((nh, count, hp), BF16),
+            V((nh, hdim, count), BF16),
+            V((lwp, 2 * rows), F32),
+            V((2, 2 * rows, lwp), BF16),
+            V((2, 2 * rows, lwp), BF16),
+            V((4, half, width), F32),
+            V((4, half, width), BF16),
+            V((4, half, width), BF16),
+            V((4, rows, width), BF16),
+            V((rows, hidden), F32),
+            V((width // 128, rows, 128), F32),
+            pltpu.SemaphoreType.DMA((7,)),
+            pltpu.SemaphoreType.DMA((16,)),
+            pltpu.SemaphoreType.DMA((16,)),
+        ],
+        compiler_params=pltpu.CompilerParams(
+            collective_id=0, has_side_effects=True, vmem_limit_bytes=60 * 1024 * 1024
+        ),
+    )(patches, pos_ids, jnp.asarray(inv), norm_gain, norm_bias, wq, qkv_bias, proj_weight, proj_bias,
+      merge_gain, merge_bias, fc1_weight, fc1_bias)
 
 
 def layer_norm(values, gain, bias):
@@ -110,8 +422,9 @@
 
 
 def solution(mesh):
+    body = fused if mesh.shape["sp"] == 4 else per_device
     return jax.shard_map(
-        per_device,
+        body,
         mesh=mesh,
         in_specs=(
             P(("img", "sp"), None),

time: 106 us -> 42.9 us (0.40)
  waiting for transfers between devices: 47.5 us -> 0 us
  Pallas kernels: 0 us -> 38.5 us
  matrix products: 21 us -> 0 us
  between operations: 13.9 us -> 0.64 us
  blocking collectives: 13 us -> 0 us
  other arithmetic: 6.95 us -> 0 us
    all_gather x3 -> x0, waiting for transfers between devices: 46.8 us -> none  [the longest x1 18.3 us: per_device(): lax.all_gather(blocks, 'sp', axis=0, tiled=True)]
    pallas_call x0 -> x1, Pallas kernels: none -> 38.5 us  [fused(): pl.pallas_call(functools.partial(fused_kernel, hdim), out_shape=(jax.Shap...]
    dot_general x4 -> x0, matrix products: 17.6 us -> none  [the longest x1 9.06 us: per_device(): jnp.dot(lax.all_gather(blocks, 'sp', axis=0, tiled=True), fc1_weight, pre...]
    all_to_all x1 -> x0, blocking collectives: 13 us -> none  [per_device(): lax.all_to_all(attended, 'sp', split_axis=0, concat_axis=1, tiled=True)]
    sub x1 -> x0, matrix products: 3.44 us -> none  [one_block(): expo = jnp.exp(scores - top)]
    convert_element_type x4 -> x0, other arithmetic: 3.4 us -> none  [the longest x1 1.98 us: per_device(): normed = layer_norm(xfloat, norm_gain, norm_bias).astype(jnp.bfloat16)]
    unnamed x16 -> x2, local copies, waits for them, and re-layouts: 0.05 us -> 3.44 us
    reduce_sum x3 -> x0, other arithmetic: 2.69 us -> none  [the longest x2 1.44 us: layer_norm(): var = jnp.mean(centered * centered, axis=-1, keepdims=True)]
  transfers between devices with their start and end apart: 3 -> 0, of which waited for: 3 -> 0; matrix products, arithmetic and copies ran while one was open for 12% -> 0% of each run, Pallas kernels for 0% -> 0%
where the time goes in v1:
time: 42.9 us; the launch traced here: 42.6 us
  Pallas kernels  38.5 us (90%)
  local copies, waits for them, and re-layouts  3.44 us (8%)
  between operations  0.64 us (1%)
    pallas_call x1, Pallas kernels, fused(): pl.pallas_call(functools.partial(fused_kernel, hdim), out_shape=(jax.Shap...  38.5 us
    unnamed x2, local copies, waits for them, and re-layouts  3.44 us

profile of v1, /device:TPU:0, one launch (start us, length us, event | category | flops | bytes accessed | tf_op | source)
XLA Modules:
  0.0 42.6 jit_solution(16806205411531322297)
XLA Ops:
  0.6 38.5 %shard_map.140 = (bf16[128,1280]{1,0:T(8,128)(2,1)}, bf16[128,1280]{1,0:T(8,128)(2,1)}) custom-call(bf16[128,1280]{1,0:T(8,128)(2,1)} %x_hbm.1, s32[2,512]{1,0:T(2,128)} %pos_ref.1, f32[128,128]{1,0:T(8,128)} %constant.2.clone.inv_ref, f32[1280]{0:T(1024)} %g1_ref.1, f32[1280]{0:T(1024)} %b1_ref.1, bf16[960,1280]{1,0:T(8,128)(2,1)} %bitcast.3, ...), custom_call_target="tpu_custom_call" | custom-call | tf_op jit(solution)/shard_map/pallas_call | solution.py:283
  39.2 1.7 %copy.17 = bf16[128,1280]{1,0:T(8,128)(2,1)} copy(bf16[128,1280]{1,0:T(8,128)(2,1)} %get-tuple-element.4) | data formatting | bytes 655360
  40.9 1.7 %copy.18 = bf16[128,1280]{1,0:T(8,128)(2,1)} copy(bf16[128,1280]{1,0:T(8,128)(2,1)} %get-tuple-element.5) | data formatting | bytes 655360

commit v2 on v1

--- a/solution.py
+++ b/solution.py
@@ -12,6 +12,7 @@
 MESH = pl.DeviceIdType.MESH
 F32 = jnp.float32
 BF16 = jnp.bfloat16
+VM_LIMIT = 56 * 1024 * 1024
 
 
 def norm_rows(v, gain, bias):
@@ -37,6 +38,7 @@
     loc, snd, rcv,
 ):
     me = lax.axis_index("sp")
+    scale = np.float32(np.log2(np.e) / np.sqrt(hdim))
     chip = me // 2
     core = me % 2
     partner = {"sp": me + 1 - 2 * core}
@@ -110,6 +112,8 @@
     lwp = att_t.shape[0]
     bias_t = jnp.transpose(bqt[:, 0:lwp])
     att_t[...] = jnp.zeros(att_t.shape, F32)
+    for h in range(nh):
+        vs[h, hdim:] = jnp.ones((vs.shape[1] - hdim, count), BF16)
     pw[0, lw:lwp] = jnp.zeros((lwp - lw, width), BF16)
     pw[1, lw:lwp] = jnp.zeros((lwp - lw, width), BF16)
     hid[...] = jnp.zeros(hid.shape, F32)
@@ -139,21 +143,22 @@
                 a = res[h * hdim:h * hdim + th]
                 b = res[h * hdim + th:(h + 1) * hdim]
                 if c == 2:
-                    vs[h, :, s * cols:(s + 1) * cols] = res[h * hdim:(h + 1) * hdim].astype(BF16)
+                    vs[h, 0:hdim, s * cols:(s + 1) * cols] = res[h * hdim:(h + 1) * hdim].astype(BF16)
                     continue
                 full = jnp.concatenate(
                     [a * cos - b * sin, b * cos + a * sin, jnp.zeros((hp - hdim, cols), F32)], axis=0
                 )
                 if c == 0:
-                    for m in range(2):
-                        qs[m, h, :, s * rows:(s + 1) * rows] = full[:, m * rows:(m + 1) * rows].astype(BF16)
+                    full = full * scale
+                    for k in range(4):
+                        qs[k, h, :, s * half:(s + 1) * half] = full[:, k * half:(k + 1) * half].astype(BF16)
                 else:
                     ks[h, s * cols:(s + 1) * cols] = jnp.transpose(full).astype(BF16)
 
     norm_half(0, 0)
     norm_half(0, 1)
     lp.wait()
-    p_send = remote(pw.at[0, pl.ds(0, lw)], pw.at[1, pl.ds(0, lw)], 7, partner)
+    p_send = remote(pw.at[0, pl.ds(0, lw)], pw.at[1, pl.ds(0, lw)], 9, partner)
     p_send.start()
     x_part.wait_recv()
     norm_half(1, 0)
@@ -164,59 +169,58 @@
         x_half[h].wait_recv()
         fwd[h].start()
         norm_half(2, h)
-    for h in range(2):
         fwd[h].wait_recv()
         norm_half(3, h)
     qkv_side(1)
 
-    scale = 1.0 / np.sqrt(np.float32(hdim))
-
     def att_copy(m):
         return remote(att.at[m], att_in.at[m], 5 + m, partner)
 
-    def attend(m, _):
+    def attend(m):
         for h in range(nh):
-            s = jnp.dot(ks[h], qs[m, h], preferred_element_type=F32) * scale
-            e = jnp.exp(s - jnp.max(s, axis=0, keepdims=True))
-            w = (e / jnp.sum(e, axis=0, keepdims=True)).astype(BF16)
-            att_t[h * hdim:(h + 1) * hdim] = jnp.dot(vs[h], w, preferred_element_type=F32)
+            s = jnp.dot(ks[h], qs[m, h], preferred_element_type=F32)
+            e = jnp.exp2(s - jnp.max(s, axis=0, keepdims=True)).astype(BF16)
+            av = jnp.dot(vs[h], e, preferred_element_type=F32)
+            att_t[h * hdim:(h + 1) * hdim] = av[0:hdim] * (1.0 / av[hdim:hdim + 1])
         att[m] = jnp.transpose(att_t[...]).astype(BF16)
         att_copy(m).start()
-        return 0
-
-    lax.fori_loop(0, 2, attend, 0)
+
     p_send.wait_recv()
 
     def part_copy(k):
-        return remote(ps.at[k], pr.at[k], 8 + k, peer)
-
-    def project(k, _):
-        m = k // 2
-
-        @pl.when(k % 2 == 0)
-        def _():
-            att_copy(m).wait_recv()
-
-        base = (k % 2) * half + core * quad
-        near = pl.ds(pl.multiple_of(base, quad), quad)
-        far = pl.ds(pl.multiple_of(rows + base, quad), quad)
-        mine = jnp.concatenate([att[m, near], att[m, far]], axis=0)
-        theirs = jnp.concatenate([att_in[m, near], att_in[m, far]], axis=0)
+        return remote(ps.at[k], pr.at[k], 10 + k, peer)
+
+    def project(k):
+        att_copy(k).wait_recv()
+        near = pl.ds(pl.multiple_of(core * quad, quad), quad)
+        far = pl.ds(pl.multiple_of(half + core * quad, quad), quad)
+        mine = jnp.concatenate([att[k, near], att[k, far]], axis=0)
+        theirs = jnp.concatenate([att_in[k, near], att_in[k, far]], axis=0)
         res = jnp.dot(mine, pw[0], preferred_element_type=F32) + jnp.dot(theirs, pw[1], preferred_element_type=F32)
         pf[k] = res
         ps[k, pl.ds(pl.multiple_of(chip * quad, quad), quad)] = res[0:quad].astype(BF16)
         ps[k, pl.ds(pl.multiple_of((1 - chip) * quad, quad), quad)] = res[quad:].astype(BF16)
         part_copy(k).start()
+
+    def mid(i, _):
+        @pl.when(i < 4)
+        def _():
+            attend(i)
+
+        @pl.when(i > 0)
+        def _():
+            project(i - 1)
+
         return 0
 
-    lax.fori_loop(0, 4, project, 0)
+    lax.fori_loop(0, 5, mid, 0)
     pb = pb_ref[...].reshape(1, width)
     g2 = g2_ref[...].reshape(1, width)
     b2 = b2_ref[...].reshape(1, width)
 
     def z_copy(k):
         mine = pl.ds(pl.multiple_of(core * half, half), half)
-        return remote(zb.at[k, mine], zb.at[k, mine], 12 + k, partner)
+        return remote(zb.at[k, mine], zb.at[k, mine], 14 + k, partner)
 
     def finish(k, _):
         @pl.when(k < 4)
@@ -254,11 +258,18 @@
     p_send.wait_send()
     for c in x_half + fwd:
         c.wait_send()
-    for m in range(2):
-        att_copy(m).wait_send()
     for k in range(4):
+        att_copy(k).wait_send()
         part_copy(k).wait_send()
         z_copy(k).wait_send()
+
+
+def put_out(vit, merged, vit_out, merged_out, sems):
+    outs = [pltpu.make_async_copy(vit, vit_out, sems.at[0]), pltpu.make_async_copy(merged, merged_out, sems.at[1])]
+    for o in outs:
+        o.start()
+    for o in outs:
+        o.wait()
 
 
 def fused(patches, pos_ids, norm_gain, norm_bias, qkv_weight, qkv_bias, proj_weight, proj_bias,
@@ -280,9 +291,9 @@
     vm = pl.BlockSpec(memory_space=pltpu.VMEM)
     hbm = pl.BlockSpec(memory_space=pl.ANY)
     V = pltpu.VMEM
-    return pl.pallas_call(
+    vit, merged = pl.pallas_call(
         functools.partial(fused_kernel, hdim),
-        out_shape=(jax.ShapeDtypeStruct((rows, width), BF16), jax.ShapeDtypeStruct((rows, hidden), BF16)),
+        out_shape=(V((rows, width), BF16), V((rows, hidden), BF16)),
         in_specs=[hbm, vm, vm, vm, vm, hbm, vm, hbm, vm, vm, vm, hbm, vm],
         out_specs=(vm, vm),
         scratch_shapes=[
@@ -295,12 +306,12 @@
             V((4, fc1_weight.shape[0] // 4, hidden), BF16),
             V((2, hdim // 2, count), F32),
             V((128, width), F32),
-            V((2, nh, hp, 2 * rows), BF16),
+            V((4, nh, hp, rows), BF16),
             V((nh, count, hp), BF16),
-            V((nh, hdim, count), BF16),
-            V((lwp, 2 * rows), F32),
-            V((2, 2 * rows, lwp), BF16),
-            V((2, 2 * rows, lwp), BF16),
+            V((nh, hdim + 16, count), BF16),
+            V((lwp, rows), F32),
+            V((4, rows, lwp), BF16),
+            V((4, rows, lwp), BF16),
             V((4, half, width), F32),
             V((4, half, width), BF16),
             V((4, half, width), BF16),
@@ -308,14 +319,22 @@
             V((rows, hidden), F32),
             V((width // 128, rows, 128), F32),
             pltpu.SemaphoreType.DMA((7,)),
-            pltpu.SemaphoreType.DMA((16,)),
-            pltpu.SemaphoreType.DMA((16,)),
+            pltpu.SemaphoreType.DMA((18,)),
+            pltpu.SemaphoreType.DMA((18,)),
         ],
         compiler_params=pltpu.CompilerParams(
-            collective_id=0, has_side_effects=True, vmem_limit_bytes=60 * 1024 * 1024
+            collective_id=0, has_side_effects=True, vmem_limit_bytes=VM_LIMIT
         ),
     )(patches, pos_ids, jnp.asarray(inv), norm_gain, norm_bias, wq, qkv_bias, proj_weight, proj_bias,
       merge_gain, merge_bias, fc1_weight, fc1_bias)
+    return pl.pallas_call(
+        put_out,
+        out_shape=(jax.ShapeDtypeStruct(vit.shape, BF16), jax.ShapeDtypeStruct(merged.shape, BF16)),
+        in_specs=[vm, vm],
+        out_specs=(hbm, hbm),
+        scratch_shapes=[pltpu.SemaphoreType.DMA((2,))],
+        compiler_params=pltpu.CompilerParams(vmem_limit_bytes=2 * 1024 * 1024),
+    )(vit, merged)
 
 
 def layer_norm(values, gain, bias):

time: 42.9 us -> 38.1 us (0.89)
  local copies, waits for them, and re-layouts: 3.44 us -> 0 us
  Pallas kernels: 38.5 us -> 37.3 us
    unnamed x2 -> x0, local copies, waits for them, and re-layouts: 3.44 us -> none
    pallas_call x1 -> x2, Pallas kernels: 38.5 us -> 37.3 us  [the longest x1 36.4 us: fused(): pl.pallas_call(functools.partial(fused_kernel, hdim), out_shape=(V((rows,...]
where the time goes in v2:
time: 38.1 us; the launch traced here: 37.9 us
  Pallas kernels  37.3 us (98%)
  between operations  0.64 us (2%)
    pallas_call x1, Pallas kernels, fused(): pl.pallas_call(functools.partial(fused_kernel, hdim), out_shape=(V((rows,...  36.4 us
    pallas_call x1, Pallas kernels, fused(): pl.pallas_call(put_out, out_shape=(jax.ShapeDtypeStruct(vit.shape, BF16),...  0.85 us

profile of v2, /device:TPU:0, one launch (start us, length us, event | category | flops | bytes accessed | tf_op | source)
XLA Modules:
  0.0 37.9 jit_solution(9867407329699031981)
XLA Ops:
  0.6 36.4 %shard_map.140 = (bf16[128,1280]{1,0:T(8,128)(2,1)S(1)}, bf16[128,1280]{1,0:T(8,128)(2,1)S(1)}) custom-call(bf16[128,1280]{1,0:T(8,128)(2,1)} %x_hbm.1, s32[2,512]{1,0:T(2,128)} %pos_ref.1, f32[128,128]{1,0:T(8,128)} %constant.2.clone.inv_ref, f32[1280]{0:T(1024)} %g1_ref.1, f32[1280]{0:T(1024)} %b1_ref.1, bf16[960,1280]{1,0:T(8,128)(2,1)} %bitcast.3, ...), custom_call_target="tpu_custom_call" | custom-call | tf_op jit(solution)/shard_map/pallas_call | solution.py:294
  37.1 0.9 %shard_map.141 = (bf16[128,1280]{1,0:T(8,128)(2,1)}, bf16[128,1280]{1,0:T(8,128)(2,1)}) custom-call(bf16[128,1280]{1,0:T(8,128)(2,1)S(1)} %get-tuple-element.4.vit, bf16[128,1280]{1,0:T(8,128)(2,1)S(1)} %get-tuple-element.5.merged), custom_call_target="tpu_custom_call" | custom-call | tf_op jit(solution)/shard_map/pallas_call | solution.py:330
